TPU v7x, 32 devices: a whole 2x2x4 slice. The times are simulated.
32 devices in a mesh: rows: 8 (over z, y), grp: 4 (over x, core).
Axes of the slice: x: 2, y: 2, z: 4, core: 2. Of those that a mesh axis runs over, the one named last changes fastest.
Arguments:
- owner: int32 [1024, 24, 3], P('rows', 'grp'), may hold values from 0 to 7, as said below
- offset: int32 [1024, 24, 3], P('rows', 'grp'), may hold values from 0 to 511
- tables: float32 [12, 4096, 128], P('grp', 'rows'), may hold values from -6 to 6
- w_first: bfloat16 [3072, 1024], P('grp'), may hold values from -0.109375 to 0.109375
- b_first: float32 [1024], replicated, may hold values from -3 to 3
- w_out: float32 [1024], replicated, may hold values from -0.1875 to 0.1875
- labels: int32 [1024], P('rows'), may hold values 0 or 1
Outputs:
- table_grad: float32 [12, 4096, 128], P('grp', 'rows')
- losses: float32 [1024], P(('rows', 'grp'))
Inputs may be any that keep to these rules, and one draw needn't show every extreme that they name: Of the lookups of one device (its 128 samples and 6 features, all three hashes) at most 1032 name one owner, and in every draw some owner gets exactly 1032. Among the lookups of one device to one owner for one table, at most 114 distinct offsets occur, and that bound is reached in every draw.
All inputs are finite; a program needn't handle non-finite values. No bound on the sum of `labels` on one device may be relied on, other than what follows from the above.
Results may differ from a plain program's by a relative error of at most 0.005.
Values may be sent and summed in bfloat16 or wider, within the bound.
A program may use at most 64 MiB of HBM per device.

v0:
```python
import functools

import jax
import jax.numpy as jnp
from jax import lax
from jax.experimental import pallas as pl
from jax.experimental.pallas import tpu as pltpu
from jax.sharding import PartitionSpec as P

BF16 = jnp.bfloat16
F32 = jnp.float32


def iota(shape, dim):
    return lax.broadcasted_iota(jnp.int32, shape, dim)


def ones_where(mask):
    return jnp.where(mask, 1.0, 0.0).astype(BF16)


def join_bands(bands, starts, width, total):
    cuts = sorted({0, total, *starts, *(min(s + width, total) for s in starts)})
    pieces = []
    for lo, hi in zip(cuts[:-1], cuts[1:]):
        piece = None
        for band, s in zip(bands, starts):
            if s <= lo and hi <= s + width:
                part = band[lo - s : hi - s]
                piece = part if piece is None else piece + part
        pieces.append(piece)
    return jnp.concatenate(pieces, axis=0).astype(BF16)


def mm(a, b):
    return jnp.dot(a, b, preferred_element_type=F32)


def kernel(
    R, G, cap, fgrp, starts, width,
    own_ref, off_ref, lab_ref, tab_hbm, w_hbm, b_ref, wo_ref,
    tg_ref, loss_ref,
    idx_ref, tab, tb, w, col, of, ranked_bf, req_send, req_recv, fet_send, rows, looked,
    p_ref, pt_ref, st_ref, part_f32, part_send, swap_recv, pair_send, pair_recv, gp, rg, g_send, g_recv,
    local_sem, ss0, rs0, ss1, rs1, ss2, rs2, ssp, rsp, ssg, rsg,
):
    me = lax.axis_index("rows")
    mg = lax.axis_index("grp")
    n_rows = tab.shape[1]
    emb = tab.shape[2]
    nl = idx_ref.shape[1]
    per = nl // 3
    bdev = per // fgrp
    share = bdev // G
    r8 = R * 8
    slots = R * width

    total = fet_send.shape[1]
    joined = functools.partial(join_bands, starts=starts, width=width, total=total)
    barrier = pltpu.get_barrier_semaphore()

    def up(k):
        return lax.rem(me + k, R)

    def down(k):
        return lax.rem(me - k + R, R)

    def gup(k):
        return lax.rem(mg + k, G)

    @pl.loop(1, R)
    def _(k):
        pl.semaphore_signal(barrier, inc=1, device_id={"rows": up(k)})

    @pl.loop(1, G)
    def _(k):
        pl.semaphore_signal(barrier, inc=1, device_id={"grp": gup(k)})

    tab_copy = pltpu.make_async_copy(tab_hbm, tab, local_sem.at[0])
    w_copy = pltpu.make_async_copy(w_hbm, w, local_sem.at[1])
    tab_copy.start()
    w_copy.start()

    idx_ref[...] = jnp.zeros_like(idx_ref)
    idx_ref[2:3, 0:bdev] = lab_ref[...]
    for t in range(3):
        for f in range(fgrp):
            lanes = pl.ds(t * per + f * bdev, bdev)
            owner = own_ref[f, t : t + 1, :]
            idx_ref[0:1, lanes] = owner * 8 + t
            idx_ref[1:2, lanes] = off_ref[f, t : t + 1, :]
            idx_ref[3:4, lanes] = owner * width + (t * (cap // 3) - starts[t])
    for j in range(nl // 128):
        col[pl.ds(j * 128, 128), :] = idx_ref[:, pl.ds(j * 128, 128)].T
    for t in range(3):
        at = pl.ds(t * per, per)
        of[at, :] = ones_where(iota((per, n_rows), 1) == col[at, 1:2])
    owner_hot = ones_where(iota((r8, nl), 0) == idx_ref[0:1, :])
    present = mm(owner_hot, of[...]) > 0.5
    before = ones_where(iota((n_rows, n_rows), 0) < iota((n_rows, n_rows), 1))
    ranked = jnp.where(present, mm(ones_where(present), before), -1.0)
    ranked_bf[...] = ranked.astype(BF16)
    req_send[...] = ranked.reshape(R, 8, n_rows)

    pl.semaphore_wait(barrier, R - 1 + G - 1)

    def req_copy(k):
        return pltpu.make_async_remote_copy(
            req_send.at[up(k)], req_recv.at[me], ss0.at[k], rs0.at[k],
            device_id={"rows": up(k)}, device_id_type=pl.DeviceIdType.MESH,
        )

    @pl.loop(1, R)
    def _(k):
        req_copy(k).start()

    tab_copy.wait()
    tb[...] = tab[...].astype(BF16)
    req_recv[me] = req_send[me]

    for t in range(3):
        at = pl.ds(t * per, per)
        own_hot = ones_where(iota((per, r8), 1) == col[at, 0:1])
        picked = mm(own_hot, ranked_bf[...]) * of[at, :].astype(F32)
        slot = jnp.sum(picked, axis=1, keepdims=True) + col[at, 3:4].astype(F32)
        looked[t] = jnp.broadcast_to(slot, (per, emb))

    def fetch(src):
        rank = req_recv[src]
        bands = []
        for t in range(3):
            shift = t * (cap // 3) - starts[t]
            line = (iota((width, n_rows), 0) - shift).astype(F32)
            line = jnp.where(line < 0.0, -2.0, line)
            bands.append(mm(ones_where(line == rank[t : t + 1, :]), tb[t]))
        fet_send[src] = joined(bands)

    def row_copy(k):
        return pltpu.make_async_remote_copy(
            fet_send.at[down(k)], rows.at[me], ss1.at[k], rs1.at[k],
            device_id={"rows": down(k)}, device_id_type=pl.DeviceIdType.MESH,
        )

    @pl.loop(1, R)
    def _(k):
        req_copy(k).wait_recv()
        fetch(down(k))
        row_copy(k).start()

    fetch(me)
    rows[me] = fet_send[me]

    lane_slot = iota((per, slots), 1).astype(F32)
    for t in range(3):
        slot = looked[t]
        p_ref[t] = ones_where(lane_slot == slot[:, 0:1])
        slot_row = slot.T[0:1, :]
        pt_ref[t] = ones_where(iota((slots, per), 0).astype(F32) == slot_row)
    req_cols = req_recv[...].reshape(r8, n_rows).T.astype(BF16)
    row_i = iota((r8, slots), 0)
    col_j = iota((r8, slots), 1)
    first = (row_i >> 3) * width
    slot_in = iota((n_rows, slots), 1) & (width - 1)
    for t in range(3):
        spread = ones_where(((row_i & 7) == t) & (col_j >= first) & (col_j < first + width))
        line = (slot_in - (t * (cap // 3) - starts[t])).astype(F32)
        line = jnp.where(line < 0.0, -2.0, line)
        st_ref[t] = ones_where(mm(req_cols, spread) == line)

    @pl.loop(1, R)
    def _(k):
        row_copy(k).wait_recv()

    for t in range(3):
        looked[t] = mm(p_ref[t], rows[:, starts[t] : starts[t] + width].reshape(slots, emb))
    embedded = (looked[0] * looked[1] + looked[2]).astype(BF16)
    features = jnp.concatenate(
        [embedded[f * bdev : (f + 1) * bdev] for f in range(fgrp)], axis=1
    )
    w_copy.wait()
    partial = mm(features, w[...])
    hidden = partial.shape[1]
    half = G // 2
    side = lax.rem(mg, 2)
    partner = mg + 1 - 2 * side
    mine = lax.div(mg, 2)
    for g in range(G):
        block = partial[g * share : (g + 1) * share]
        part_f32[g % 2, g // 2] = block
        part_send[g % 2, g // 2] = block.astype(BF16)
    swap = pltpu.make_async_remote_copy(
        part_send.at[1 - side], swap_recv, ssp.at[0], rsp.at[0],
        device_id={"grp": partner}, device_id_type=pl.DeviceIdType.MESH,
    )
    swap.start()

    def part_copy(k):
        peer = lax.rem(mg + 2 * k, G)
        return pltpu.make_async_remote_copy(
            pair_send, pair_recv.at[k], ssp.at[k], rsp.at[k],
            device_id={"grp": peer}, device_id_type=pl.DeviceIdType.MESH,
        )

    swap.wait_recv()
    pair = part_f32[side] + swap_recv[...].astype(F32)
    pair_send[...] = pair.astype(BF16)
    for k in range(1, half):
        part_copy(k).start()
    pair = pair + b_ref[...]
    for k in range(1, half):
        part_copy(k).wait_recv()
        pair = pair + pair_recv[k].astype(F32)
    pre = pair.reshape(half * share, hidden)
    sig = jax.nn.sigmoid(pre)
    w_out = wo_ref[...]
    logits = jnp.sum(pre * sig * w_out, axis=1, keepdims=True)
    targets = jnp.concatenate(
        [
            col[pl.ds(pl.multiple_of((2 * j + side) * share, share), share), 2:3]
            for j in range(half)
        ],
        axis=0,
    ).astype(F32)
    grad_logit = jax.nn.sigmoid(logits) - targets
    grad_half = (grad_logit * w_out * (sig * (1.0 + pre * (1.0 - sig)))).astype(BF16)
    gp[side] = grad_half.reshape(half, share, hidden)
    gp_copy = pltpu.make_async_remote_copy(
        gp.at[side], gp.at[side], ssg.at[0], rsg.at[0],
        device_id={"grp": partner}, device_id_type=pl.DeviceIdType.MESH,
    )
    gp_copy.start()
    losses = (
        jnp.maximum(logits, 0.0) + jnp.log1p(jnp.exp(-jnp.abs(logits))) - targets * logits
    )
    diag = iota((half * share, share), 0) - mine * share == iota((half * share, share), 1)
    loss_ref[...] = jnp.sum(jnp.where(diag, losses, 0.0), axis=0, keepdims=True)
    gp_copy.wait_recv()
    grad_pre = jnp.concatenate([gp[g % 2, g // 2] for g in range(G)], axis=0)

    grad_emb = lax.dot_general(
        grad_pre, w[...], (((1,), (1,)), ((), ())),
        preferred_element_type=F32,
    )
    grad_rows = jnp.concatenate(
        [grad_emb[:, f * emb : (f + 1) * emb] for f in range(fgrp)], axis=0
    )
    rg[0] = (grad_rows * looked[1]).astype(BF16)
    rg[1] = (grad_rows * looked[0]).astype(BF16)
    rg[2] = grad_rows.astype(BF16)

    def collect(dst):
        at = pl.ds(pl.multiple_of(dst * width, width), width)
        g_send[dst] = joined([mm(pt_ref[t, at, :], rg[t]) for t in range(3)])

    def grad_copy(k):
        return pltpu.make_async_remote_copy(
            g_send.at[up(k)], g_recv.at[me], ss2.at[k], rs2.at[k],
            device_id={"rows": up(k)}, device_id_type=pl.DeviceIdType.MESH,
        )

    @pl.loop(1, R)
    def _(k):
        collect(up(k))
        grad_copy(k).start()

    collect(me)
    g_recv[me] = g_send[me]

    @pl.loop(1, R)
    def _(k):
        req_copy(k).wait_send()
        row_copy(k).wait_send()

    swap.wait_send()
    gp_copy.wait_send()
    for k in range(1, half):
        part_copy(k).wait_send()

    @pl.loop(1, R)
    def _(k):
        grad_copy(k).wait_recv()

    for t in range(3):
        tg_ref[t] = mm(st_ref[t], g_recv[:, starts[t] : starts[t] + width].reshape(slots, emb))

    @pl.loop(1, R)
    def _(k):
        grad_copy(k).wait_send()


def body(owner, offset, tables, w_first, b_first, w_out, labels):
    R, G = lax.axis_size("rows"), lax.axis_size("grp")
    bdev, fgrp = owner.shape[0], owner.shape[1]
    n_rows, emb = tables.shape[1], tables.shape[2]
    hidden = w_first.shape[1]
    per = bdev * fgrp
    nl = 3 * per
    hot_count = 8 * (per * 7 // (16 * R)) + 8
    uniq = hot_count // 3
    cap = 3 * uniq
    total = -(-cap // 16) * 16
    starts = [t * uniq // 16 * 16 for t in range(3)]
    width = 16
    while any(s + width < (t + 1) * uniq for t, s in enumerate(starts)):
        width *= 2
    total = max(total, max(starts) + width)
    share = bdev // G
    half = G // 2
    slots = R * width

    owner_rows = owner.transpose(1, 2, 0)
    offset_rows = offset.transpose(1, 2, 0)
    vmem = pl.BlockSpec(memory_space=pltpu.VMEM)
    hbm = pl.BlockSpec(memory_space=pl.ANY)
    sems = pltpu.SemaphoreType.DMA
    table_grad, losses = pl.pallas_call(
        functools.partial(kernel, R, G, cap, fgrp, starts, width),
        out_shape=(
            jax.ShapeDtypeStruct((3, n_rows, emb), F32),
            jax.ShapeDtypeStruct((1, share), F32),
        ),
        in_specs=[vmem, vmem, vmem, hbm, hbm, vmem, vmem],
        out_specs=(vmem, vmem),
        scratch_shapes=[
            pltpu.VMEM((8, nl), jnp.int32),
            pltpu.VMEM((3, n_rows, emb), F32),
            pltpu.VMEM((3, n_rows, emb), BF16),
            pltpu.VMEM(w_first.shape, BF16),
            pltpu.VMEM((nl, 8), jnp.int32),
            pltpu.VMEM((nl, n_rows), BF16),
            pltpu.VMEM((R * 8, n_rows), BF16),
            pltpu.VMEM((R, 8, n_rows), F32),
            pltpu.VMEM((R, 8, n_rows), F32),
            pltpu.VMEM((R, total, emb), BF16),
            pltpu.VMEM((R, total, emb), BF16),
            pltpu.VMEM((3, per, emb), F32),
            pltpu.VMEM((3, per, slots), BF16),
            pltpu.VMEM((3, slots, per), BF16),
            pltpu.VMEM((3, n_rows, slots), BF16),
            pltpu.VMEM((2, half, share, hidden), F32),
            pltpu.VMEM((2, half, share, hidden), BF16),
            pltpu.VMEM((half, share, hidden), BF16),
            pltpu.VMEM((half, share, hidden), BF16),
            pltpu.VMEM((half, half, share, hidden), BF16),
            pltpu.VMEM((2, half, share, hidden), BF16),
            pltpu.VMEM((3, per, emb), BF16),
            pltpu.VMEM((R, total, emb), BF16),
            pltpu.VMEM((R, total, emb), BF16),
            sems((2,)),
            sems((R,)), sems((R,)), sems((R,)), sems((R,)), sems((R,)), sems((R,)),
            sems((G,)), sems((G,)), sems((G,)), sems((G,)),
        ],
        compiler_params=pltpu.CompilerParams(
            collective_id=0, has_side_effects=True, vmem_limit_bytes=60 * 1024 * 1024
        ),
        name="embed_step",
    )(owner_rows, offset_rows, labels.reshape(1, bdev), tables, w_first, b_first.reshape(1, hidden), w_out.reshape(1, hidden))
    return table_grad, losses.reshape(share)


def solution(mesh):
    placed = (
        P("rows", "grp", None),
        P("rows", "grp", None),
        P("grp", "rows", None),
        P("grp", None),
        P(),
        P(),
        P("rows"),
    )
    return jax.shard_map(
        body,
        mesh=mesh,
        in_specs=placed,
        out_specs=(P("grp", "rows", None), P(("rows", "grp"))),
        check_vma=False,
    )
```

profile of v0, /device:TPU:13, one launch (start us, length us, event | category | flops | bytes accessed | tf_op | source)
XLA Modules:
  0.0 57.0 jit_solution(14182422313117472176)
XLA Ops:
  0.6 53.7 %embed_step.1 = (f32[3,512,128]{2,1,0:T(8,128)}, f32[1,32]{1,0:T(1,128)}) custom-call(s32[6,3,128]{2,1,0:T(4,128)} %bitcast.6, s32[6,3,128]{2,1,0:T(4,128)} %bitcast.7, s32[1,128]{1,0:T(1,128)} %bitcast.10, f32[3,512,128]{2,1,0:T(8,128)} %tab_hbm.1, bf16[768,1024]{1,0:T(8,128)(2,1)} %w_hbm.1, f32[1,1024]{1,0:T(1,128)} %bitcast.8, f32[1,1024]{1,0:T(1,128)} %bitcast.9), custom_call_target="tpu_custom_call" | custom-call | tf_op jit(solution)/shard_map/embed_step/pallas_call | solution.py:316
  54.4 0.0 copy-start
  54.4 2.1 %copy.11 = f32[3,512,128]{2,1,0:T(8,128)} copy(f32[3,512,128]{2,1,0:T(8,128)} %get-tuple-element.8) | data formatting | bytes 1572864
  56.4 0.0 copy-done
  56.4 0.5 copy.12
Async XLA Ops:
  54.4 2.1 %copy-start = (f32[1,32]{1,0:T(1,128)S(1)}, f32[1,32]{1,0:T(1,128)}, u32[]{:S(2)}) copy-start(f32[1,32]{1,0:T(1,128)} %get-tuple-element.5) | copy-start | bytes 388
where the time goes:
time: 57.2 us; the launch traced here: 57 us
  Pallas kernels  53.7 us (94%)
  local copies, waits for them, and re-layouts  2.58 us (5%)
  between operations  0.65 us (1%)
    pallas_call x1, Pallas kernels, body(): pl.pallas_call(functools.partial(kernel, R, G, cap, fgrp, starts, width),...  53.7 us
    unnamed x4, local copies, waits for them, and re-layouts  2.58 us

commit v1 on v0

--- a/solution.py
+++ b/solution.py
@@ -9,6 +9,9 @@
 
 BF16 = jnp.bfloat16
 F32 = jnp.float32
+CHUNKS = 4
+ORDER = (0, 1, 3, 2)
+MIB = 1024 * 1024
 
 
 def iota(shape, dim):
@@ -54,6 +57,11 @@
     share = bdev // G
     r8 = R * 8
     slots = R * width
+    fan = R // CHUNKS
+    chunk = fan * width
+    my_chunk = lax.div(me, fan)
+    side_of = lax.rem(me, fan)
+    sent = -(-cap // 8) * 8
 
     total = fet_send.shape[1]
     joined = functools.partial(join_bands, starts=starts, width=width, total=total)
@@ -67,6 +75,50 @@
 
     def gup(k):
         return lax.rem(mg + k, G)
+
+    def nth_chunk(n):
+        return lax.rem(my_chunk + ORDER[n], CHUNKS)
+
+    def exchange(make, send, recv, ss, rs, target):
+        used = pl.ds(0, sent)
+
+        def copy(k):
+            return pltpu.make_async_remote_copy(
+                send.at[target(k), used], recv.at[me, used], ss.at[k], rs.at[me],
+                device_id={"rows": target(k)}, device_id_type=pl.DeviceIdType.MESH,
+            )
+
+        def arrival(src):
+            return pltpu.make_async_remote_copy(
+                send.at[src, used], recv.at[src, used], ss.at[0], rs.at[src],
+                device_id={"rows": src}, device_id_type=pl.DeviceIdType.MESH,
+            )
+
+        def start():
+            @pl.loop(1, R)
+            def _(k):
+                make(target(k))
+                copy(k).start()
+
+            make(me)
+            recv[me] = send[me]
+
+        def wait_chunk(n):
+            if n == 0:
+                @pl.loop(1, fan)
+                def _(i):
+                    arrival(my_chunk * fan + lax.rem(side_of + i, fan)).wait_recv()
+            else:
+                @pl.loop(0, fan)
+                def _(i):
+                    arrival(nth_chunk(n) * fan + i).wait_recv()
+
+        def drain():
+            @pl.loop(1, R)
+            def _(k):
+                copy(k).wait_send()
+
+        return start, wait_chunk, drain
 
     @pl.loop(1, R)
     def _(k):
@@ -81,6 +133,8 @@
     tab_copy.start()
     w_copy.start()
 
+    for ref in (rows, g_recv):
+        ref[:, total - 16 : total] = jnp.zeros((R, 16, emb), BF16)
     idx_ref[...] = jnp.zeros_like(idx_ref)
     idx_ref[2:3, 0:bdev] = lab_ref[...]
     for t in range(3):
@@ -100,14 +154,20 @@
     before = ones_where(iota((n_rows, n_rows), 0) < iota((n_rows, n_rows), 1))
     ranked = jnp.where(present, mm(ones_where(present), before), -1.0)
     ranked_bf[...] = ranked.astype(BF16)
-    req_send[...] = ranked.reshape(R, 8, n_rows)
+    req_send[...] = ranked.reshape(R, 8, n_rows)[:, 0:4].astype(BF16)
 
     pl.semaphore_wait(barrier, R - 1 + G - 1)
 
     def req_copy(k):
         return pltpu.make_async_remote_copy(
-            req_send.at[up(k)], req_recv.at[me], ss0.at[k], rs0.at[k],
+            req_send.at[up(k)], req_recv.at[me], ss0.at[k], rs0.at[me],
             device_id={"rows": up(k)}, device_id_type=pl.DeviceIdType.MESH,
+        )
+
+    def req_arrival(src):
+        return pltpu.make_async_remote_copy(
+            req_send.at[src], req_recv.at[src], ss0.at[0], rs0.at[src],
+            device_id={"rows": src}, device_id_type=pl.DeviceIdType.MESH,
         )
 
     @pl.loop(1, R)
@@ -126,7 +186,11 @@
         looked[t] = jnp.broadcast_to(slot, (per, emb))
 
     def fetch(src):
-        rank = req_recv[src]
+        @pl.when(src != me)
+        def _():
+            req_arrival(src).wait_recv()
+
+        rank = req_recv[src].astype(F32)
         bands = []
         for t in range(3):
             shift = t * (cap // 3) - starts[t]
@@ -135,44 +199,39 @@
             bands.append(mm(ones_where(line == rank[t : t + 1, :]), tb[t]))
         fet_send[src] = joined(bands)
 
-    def row_copy(k):
-        return pltpu.make_async_remote_copy(
-            fet_send.at[down(k)], rows.at[me], ss1.at[k], rs1.at[k],
-            device_id={"rows": down(k)}, device_id_type=pl.DeviceIdType.MESH,
-        )
-
-    @pl.loop(1, R)
-    def _(k):
-        req_copy(k).wait_recv()
-        fetch(down(k))
-        row_copy(k).start()
-
-    fetch(me)
-    rows[me] = fet_send[me]
-
-    lane_slot = iota((per, slots), 1).astype(F32)
+    rows_start, rows_wait, rows_drain = exchange(fetch, fet_send, rows, ss1, rs1, down)
+    rows_start()
+
+    lane_slot = iota((per, chunk), 1).astype(F32)
+    slot_rows = []
     for t in range(3):
         slot = looked[t]
-        p_ref[t] = ones_where(lane_slot == slot[:, 0:1])
-        slot_row = slot.T[0:1, :]
-        pt_ref[t] = ones_where(iota((slots, per), 0).astype(F32) == slot_row)
-    req_cols = req_recv[...].reshape(r8, n_rows).T.astype(BF16)
-    row_i = iota((r8, slots), 0)
-    col_j = iota((r8, slots), 1)
-    first = (row_i >> 3) * width
-    slot_in = iota((n_rows, slots), 1) & (width - 1)
-    for t in range(3):
-        spread = ones_where(((row_i & 7) == t) & (col_j >= first) & (col_j < first + width))
+        for c in range(CHUNKS):
+            p_ref[t, c] = ones_where(lane_slot == slot[:, 0:1] - float(c * chunk))
+        slot_rows.append(slot.T[0:1, :])
+    for t in range(3):
+        pt_ref[t] = ones_where(iota((slots, per), 0).astype(F32) == slot_rows[t])
+    req_cols = req_recv[...].astype(F32).reshape(R * 4, n_rows).T.astype(BF16)
+    row_i = iota((R * 4, chunk), 0)
+    slot_in = iota((n_rows, chunk), 1) & (width - 1)
+    for t in range(3):
         line = (slot_in - (t * (cap // 3) - starts[t])).astype(F32)
         line = jnp.where(line < 0.0, -2.0, line)
-        st_ref[t] = ones_where(mm(req_cols, spread) == line)
-
-    @pl.loop(1, R)
-    def _(k):
-        row_copy(k).wait_recv()
-
-    for t in range(3):
-        looked[t] = mm(p_ref[t], rows[:, starts[t] : starts[t] + width].reshape(slots, emb))
+        for c in range(CHUNKS):
+            col_j = iota((R * 4, chunk), 1) + c * chunk
+            first = (row_i >> 2) * width
+            spread = ones_where(((row_i & 3) == t) & (col_j >= first) & (col_j < first + width))
+            st_ref[t, c] = ones_where(mm(req_cols, spread) == line)
+
+    def arrived(ref, n, t):
+        src = pl.ds(nth_chunk(n) * fan, fan)
+        return ref[src, starts[t] : starts[t] + width].reshape(chunk, emb)
+
+    for n in range(CHUNKS):
+        rows_wait(n)
+        for t in range(3):
+            part = mm(p_ref[t, nth_chunk(n)], arrived(rows, n, t))
+            looked[t] = part if n == 0 else looked[t] + part
     embedded = (looked[0] * looked[1] + looked[2]).astype(BF16)
     features = jnp.concatenate(
         [embedded[f * bdev : (f + 1) * bdev] for f in range(fgrp)], axis=1
@@ -252,40 +311,26 @@
         at = pl.ds(pl.multiple_of(dst * width, width), width)
         g_send[dst] = joined([mm(pt_ref[t, at, :], rg[t]) for t in range(3)])
 
-    def grad_copy(k):
-        return pltpu.make_async_remote_copy(
-            g_send.at[up(k)], g_recv.at[me], ss2.at[k], rs2.at[k],
-            device_id={"rows": up(k)}, device_id_type=pl.DeviceIdType.MESH,
-        )
-
-    @pl.loop(1, R)
-    def _(k):
-        collect(up(k))
-        grad_copy(k).start()
-
-    collect(me)
-    g_recv[me] = g_send[me]
+    g_start, g_wait, g_drain = exchange(collect, g_send, g_recv, ss2, rs2, up)
+    g_start()
 
     @pl.loop(1, R)
     def _(k):
         req_copy(k).wait_send()
-        row_copy(k).wait_send()
-
+
+    rows_drain()
     swap.wait_send()
     gp_copy.wait_send()
     for k in range(1, half):
         part_copy(k).wait_send()
 
-    @pl.loop(1, R)
-    def _(k):
-        grad_copy(k).wait_recv()
-
-    for t in range(3):
-        tg_ref[t] = mm(st_ref[t], g_recv[:, starts[t] : starts[t] + width].reshape(slots, emb))
-
-    @pl.loop(1, R)
-    def _(k):
-        grad_copy(k).wait_send()
+    for n in range(CHUNKS):
+        g_wait(n)
+        for t in range(3):
+            part = mm(st_ref[t, nth_chunk(n)], arrived(g_recv, n, t))
+            tg_ref[t] = part if n == 0 else tg_ref[t] + part
+
+    g_drain()
 
 
 def body(owner, offset, tables, w_first, b_first, w_out, labels):
@@ -329,14 +374,14 @@
             pltpu.VMEM((nl, 8), jnp.int32),
             pltpu.VMEM((nl, n_rows), BF16),
             pltpu.VMEM((R * 8, n_rows), BF16),
-            pltpu.VMEM((R, 8, n_rows), F32),
-            pltpu.VMEM((R, 8, n_rows), F32),
+            pltpu.VMEM((R, 4, n_rows), BF16),
+            pltpu.VMEM((R, 4, n_rows), BF16),
             pltpu.VMEM((R, total, emb), BF16),
             pltpu.VMEM((R, total, emb), BF16),
             pltpu.VMEM((3, per, emb), F32),
-            pltpu.VMEM((3, per, slots), BF16),
+            pltpu.VMEM((3, CHUNKS, per, slots // CHUNKS), BF16),
             pltpu.VMEM((3, slots, per), BF16),
-            pltpu.VMEM((3, n_rows, slots), BF16),
+            pltpu.VMEM((3, CHUNKS, n_rows, slots // CHUNKS), BF16),
             pltpu.VMEM((2, half, share, hidden), F32),
             pltpu.VMEM((2, half, share, hidden), BF16),
             pltpu.VMEM((half, share, hidden), BF16),
@@ -351,10 +396,18 @@
             sems((G,)), sems((G,)), sems((G,)), sems((G,)),
         ],
         compiler_params=pltpu.CompilerParams(
-            collective_id=0, has_side_effects=True, vmem_limit_bytes=60 * 1024 * 1024
+            collective_id=0, has_side_effects=True, vmem_limit_bytes=(44 if slots <= 1024 else 60) * MIB
         ),
         name="embed_step",
-    )(owner_rows, offset_rows, labels.reshape(1, bdev), tables, w_first, b_first.reshape(1, hidden), w_out.reshape(1, hidden))
+    )(
+        *(
+            pltpu.with_memory_space_constraint(v, pltpu.HBM)
+            for v in (
+                owner_rows, offset_rows, labels.reshape(1, bdev), tables, w_first,
+                b_first.reshape(1, hidden), w_out.reshape(1, hidden),
+            )
+        )
+    )
     return table_grad, losses.reshape(share)
 
 

time: 57.2 us -> 54 us (0.944)
  Pallas kernels: 53.7 us -> 51.7 us
  local copies, waits for them, and re-layouts: 2.58 us -> 1.39 us
    pallas_call x1, Pallas kernels: 53.7 us -> 51.7 us  [body(): pl.pallas_call(functools.partial(kernel, R, G, cap, fgrp, starts, width),...]
    unnamed x4 -> x2, local copies, waits for them, and re-layouts: 2.58 us -> 1.39 us
where the time goes in v1:
time: 54 us; the launch traced here: 53.7 us
  Pallas kernels  51.7 us (96%)
  local copies, waits for them, and re-layouts  1.39 us (3%)
  between operations  0.64 us (1%)
    pallas_call x1, Pallas kernels, body(): pl.pallas_call(functools.partial(kernel, R, G, cap, fgrp, starts, width),...  51.7 us
    unnamed x2, local copies, waits for them, and re-layouts  1.39 us

profile of v1, /device:TPU:13, one launch (start us, length us, event | category | flops | bytes accessed | tf_op | source)
XLA Modules:
  0.0 53.7 jit_solution(13699558128392413729)
XLA Ops:
  0.6 51.7 %embed_step.1 = (f32[3,512,128]{2,1,0:T(8,128)S(1)}, f32[1,32]{1,0:T(1,128)S(1)}) custom-call(s32[6,3,128]{2,1,0:T(4,128)} %bitcast.7, s32[6,3,128]{2,1,0:T(4,128)} %bitcast.8, s32[1,128]{1,0:T(1,128)} %bitcast.11, f32[3,512,128]{2,1,0:T(8,128)} %tab_hbm.1, bf16[768,1024]{1,0:T(8,128)(2,1)} %w_hbm.1, f32[1,1024]{1,0:T(1,128)} %bitcast.9, f32[1,1024]{1,0:T(1,128)} %bitcast.10), custom_call_target="tpu_custom_call" | custom-call | tf_op jit(solution)/shard_map/embed_step/pallas_call | solution.py:361
  52.3 0.9 %copy.11 = f32[3,512,128]{2,1,0:T(8,128)} copy(f32[3,512,128]{2,1,0:T(8,128)S(1)} %get-tuple-element.8) | data formatting | bytes 1572864
  53.2 0.5 copy.12

commit v2 on v1

--- a/solution.py
+++ b/solution.py
@@ -10,7 +10,8 @@
 BF16 = jnp.bfloat16
 F32 = jnp.float32
 CHUNKS = 4
-ORDER = (0, 1, 3, 2)
+PARTS = 2
+DENSE_AT = 1
 MIB = 1024 * 1024
 
 
@@ -43,9 +44,9 @@
     R, G, cap, fgrp, starts, width,
     own_ref, off_ref, lab_ref, tab_hbm, w_hbm, b_ref, wo_ref,
     tg_ref, loss_ref,
-    idx_ref, tab, tb, w, col, of, ranked_bf, req_send, req_recv, fet_send, rows, looked,
+    idx_ref, tab, tb, w, w_t, col, of, ranked_bf, req_send, req_recv, fet_send, rows, dense, dense_part, looked,
     p_ref, pt_ref, st_ref, part_f32, part_send, swap_recv, pair_send, pair_recv, gp, rg, g_send, g_recv,
-    local_sem, ss0, rs0, ss1, rs1, ss2, rs2, ssp, rsp, ssg, rsg,
+    local_sem, ss0, rs0, ss1, rs1, ss2, rs2, ssd, rsd, ssp, rsp, ssg, rsg,
 ):
     me = lax.axis_index("rows")
     mg = lax.axis_index("grp")
@@ -62,6 +63,7 @@
     my_chunk = lax.div(me, fan)
     side_of = lax.rem(me, fan)
     sent = -(-cap // 8) * 8
+    sent_short = starts[1] + width
 
     total = fet_send.shape[1]
     joined = functools.partial(join_bands, starts=starts, width=width, total=total)
@@ -70,55 +72,114 @@
     def up(k):
         return lax.rem(me + k, R)
 
-    def down(k):
-        return lax.rem(me - k + R, R)
-
     def gup(k):
         return lax.rem(mg + k, G)
 
+    paired = R == 2 * CHUNKS
+    my_half = lax.div(my_chunk, 2)
+    pair_chunk = my_chunk + 1 - 2 * lax.rem(my_chunk, 2)
+    far_inner = 2 - my_half
+
     def nth_chunk(n):
-        return lax.rem(my_chunk + ORDER[n], CHUNKS)
-
-    def exchange(make, send, recv, ss, rs, target):
-        used = pl.ds(0, sent)
-
-        def copy(k):
+        if not paired:
+            return lax.rem(my_chunk + n, CHUNKS)
+        return (my_chunk, pair_chunk, 3 - 3 * my_half, far_inner)[n]
+
+    def is_inner(z):
+        return lax.rem(lax.div(z + 1, 2), 2)
+
+    def same(a, b):
+        return (a == b).astype(jnp.int32)
+
+    def served(z, y, to_z, to_y):
+        across = 1 - same(lax.div(z, 2), lax.div(to_z, 2))
+        return is_inner(z) * across * (is_inner(to_z) + (1 - is_inner(to_z)) * same(y, to_y))
+
+    inner = is_inner(my_chunk)
+
+    def exchange(make, send, recv, ss, rs, shorter):
+        def copy(k, count):
             return pltpu.make_async_remote_copy(
-                send.at[target(k), used], recv.at[me, used], ss.at[k], rs.at[me],
-                device_id={"rows": target(k)}, device_id_type=pl.DeviceIdType.MESH,
+                send.at[up(k), pl.ds(0, count)], recv.at[me, pl.ds(0, count)], ss.at[k], rs.at[me],
+                device_id={"rows": up(k)}, device_id_type=pl.DeviceIdType.MESH,
             )
 
-        def arrival(src):
+        def arrival(src, count):
             return pltpu.make_async_remote_copy(
-                send.at[src, used], recv.at[src, used], ss.at[0], rs.at[src],
+                send.at[src, pl.ds(0, count)], recv.at[src, pl.ds(0, count)], ss.at[0], rs.at[src],
                 device_id={"rows": src}, device_id_type=pl.DeviceIdType.MESH,
             )
+
+        def by_size(k, act):
+            if not shorter:
+                act(copy(k, sent))
+                return
+            cut = served(my_chunk, side_of, lax.div(up(k), fan), lax.rem(up(k), fan))
+
+            @pl.when(cut == 1)
+            def _():
+                act(copy(k, sent_short))
+
+            @pl.when(cut == 0)
+            def _():
+                act(copy(k, sent))
 
         def start():
             @pl.loop(1, R)
             def _(k):
-                make(target(k))
-                copy(k).start()
+                make(up(k))
+                by_size(k, lambda c: c.start())
 
             make(me)
             recv[me] = send[me]
 
         def wait_chunk(n):
-            if n == 0:
-                @pl.loop(1, fan)
-                def _(i):
-                    arrival(my_chunk * fan + lax.rem(side_of + i, fan)).wait_recv()
-            else:
-                @pl.loop(0, fan)
-                def _(i):
-                    arrival(nth_chunk(n) * fan + i).wait_recv()
+            mixed = shorter and n == CHUNKS - 1
+
+            @pl.loop(0, fan)
+            def _(i):
+                src = nth_chunk(n) * fan + i
+
+                @pl.when(src != me)
+                def _():
+                    if not mixed:
+                        arrival(src, sent).wait_recv()
+                        return
+                    cut = served(nth_chunk(n), i, my_chunk, side_of)
+
+                    @pl.when(cut == 1)
+                    def _():
+                        arrival(src, sent_short).wait_recv()
+
+                    @pl.when(cut == 0)
+                    def _():
+                        arrival(src, sent).wait_recv()
 
         def drain():
             @pl.loop(1, R)
             def _(k):
-                copy(k).wait_send()
+                by_size(k, lambda c: c.wait_send())
 
         return start, wait_chunk, drain
+
+    def dense_copy(j):
+        dst = (
+            far_inner * fan + side_of,
+            my_chunk * fan + 1 - side_of,
+            pair_chunk * fan + side_of,
+        )[j]
+        return pltpu.make_async_remote_copy(
+            tb.at[2] if j == 0 else dense.at[side_of], dense.at[side_of], ssd.at[j], rsd.at[side_of],
+            device_id={"rows": dst}, device_id_type=pl.DeviceIdType.MESH,
+        )
+
+    def dense_wait(ys):
+        pltpu.make_async_remote_copy(
+            tb.at[2], dense.at[ys], ssd.at[0], rsd.at[ys],
+            device_id={"rows": up(1)}, device_id_type=pl.DeviceIdType.MESH,
+        ).wait_recv()
+
+    dense[...] = jnp.zeros_like(dense)
 
     @pl.loop(1, R)
     def _(k):
@@ -133,8 +194,9 @@
     tab_copy.start()
     w_copy.start()
 
-    for ref in (rows, g_recv):
-        ref[:, total - 16 : total] = jnp.zeros((R, 16, emb), BF16)
+    clear = sent_short if paired else total - 16
+    rows[:, clear:total] = jnp.zeros((R, total - clear, emb), BF16)
+    g_recv[:, total - 16 : total] = jnp.zeros((R, 16, emb), BF16)
     idx_ref[...] = jnp.zeros_like(idx_ref)
     idx_ref[2:3, 0:bdev] = lab_ref[...]
     for t in range(3):
@@ -176,14 +238,12 @@
 
     tab_copy.wait()
     tb[...] = tab[...].astype(BF16)
+    if paired:
+        @pl.when(inner == 1)
+        def _():
+            dense_copy(0).start()
+
     req_recv[me] = req_send[me]
-
-    for t in range(3):
-        at = pl.ds(t * per, per)
-        own_hot = ones_where(iota((per, r8), 1) == col[at, 0:1])
-        picked = mm(own_hot, ranked_bf[...]) * of[at, :].astype(F32)
-        slot = jnp.sum(picked, axis=1, keepdims=True) + col[at, 3:4].astype(F32)
-        looked[t] = jnp.broadcast_to(slot, (per, emb))
 
     def fetch(src):
         @pl.when(src != me)
@@ -199,8 +259,21 @@
             bands.append(mm(ones_where(line == rank[t : t + 1, :]), tb[t]))
         fet_send[src] = joined(bands)
 
-    rows_start, rows_wait, rows_drain = exchange(fetch, fet_send, rows, ss1, rs1, down)
+    rows_start, rows_wait, rows_drain = exchange(fetch, fet_send, rows, ss1, rs1, paired)
     rows_start()
+    if paired:
+        @pl.when(inner == 1)
+        def _():
+            dense_wait(side_of)
+            for j in range(1, 3):
+                dense_copy(j).start()
+
+    for t in range(3):
+        at = pl.ds(t * per, per)
+        own_hot = ones_where(iota((per, r8), 1) == col[at, 0:1])
+        picked = mm(own_hot, ranked_bf[...]) * of[at, :].astype(F32)
+        slot = jnp.sum(picked, axis=1, keepdims=True) + col[at, 3:4].astype(F32)
+        looked[t] = jnp.broadcast_to(slot, (per, emb))
 
     lane_slot = iota((per, chunk), 1).astype(F32)
     slot_rows = []
@@ -223,6 +296,10 @@
             spread = ones_where(((row_i & 3) == t) & (col_j >= first) & (col_j < first + width))
             st_ref[t, c] = ones_where(mm(req_cols, spread) == line)
 
+    w_copy.wait()
+    for f in range(fgrp):
+        w_t[:, f * emb : (f + 1) * emb] = w[f * emb : (f + 1) * emb, :].T
+
     def arrived(ref, n, t):
         src = pl.ds(nth_chunk(n) * fan, fan)
         return ref[src, starts[t] : starts[t] + width].reshape(chunk, emb)
@@ -232,47 +309,78 @@
         for t in range(3):
             part = mm(p_ref[t, nth_chunk(n)], arrived(rows, n, t))
             looked[t] = part if n == 0 else looked[t] + part
+        if paired and n == DENSE_AT:
+            at = pl.ds(2 * per, per)
+            keys = []
+            for ys in range(2):
+                used = served(far_inner, ys, my_chunk, side_of)
+
+                @pl.when(used * (1 - inner * same(side_of, ys)) == 1)
+                def _():
+                    dense_wait(ys)
+
+                key = ((far_inner * fan + ys) * 8 + 2) * used - (1 - used)
+                keys.append(key)
+                part = jnp.where(col[at, 0:1] == key, mm(of[at, :], dense[ys]), 0.0)
+                dense_part[...] = part if ys == 0 else dense_part[...] + part
+    if paired:
+        hit = (col[at, 0:1] == keys[0]) | (col[at, 0:1] == keys[1])
+        looked[2] = jnp.where(hit, dense_part[...], looked[2])
     embedded = (looked[0] * looked[1] + looked[2]).astype(BF16)
     features = jnp.concatenate(
         [embedded[f * bdev : (f + 1) * bdev] for f in range(fgrp)], axis=1
     )
-    w_copy.wait()
-    partial = mm(features, w[...])
-    hidden = partial.shape[1]
+    hidden = w.shape[1]
     half = G // 2
     side = lax.rem(mg, 2)
     partner = mg + 1 - 2 * side
     mine = lax.div(mg, 2)
-    for g in range(G):
-        block = partial[g * share : (g + 1) * share]
-        part_f32[g % 2, g // 2] = block
-        part_send[g % 2, g // 2] = block.astype(BF16)
-    swap = pltpu.make_async_remote_copy(
-        part_send.at[1 - side], swap_recv, ssp.at[0], rsp.at[0],
-        device_id={"grp": partner}, device_id_type=pl.DeviceIdType.MESH,
-    )
-    swap.start()
-
-    def part_copy(k):
-        peer = lax.rem(mg + 2 * k, G)
+
+    def swap(c):
         return pltpu.make_async_remote_copy(
-            pair_send, pair_recv.at[k], ssp.at[k], rsp.at[k],
-            device_id={"grp": peer}, device_id_type=pl.DeviceIdType.MESH,
-        )
-
-    swap.wait_recv()
-    pair = part_f32[side] + swap_recv[...].astype(F32)
-    pair_send[...] = pair.astype(BF16)
-    for k in range(1, half):
-        part_copy(k).start()
-    pair = pair + b_ref[...]
-    for k in range(1, half):
-        part_copy(k).wait_recv()
-        pair = pair + pair_recv[k].astype(F32)
-    pre = pair.reshape(half * share, hidden)
-    sig = jax.nn.sigmoid(pre)
-    w_out = wo_ref[...]
-    logits = jnp.sum(pre * sig * w_out, axis=1, keepdims=True)
+            part_send.at[c, 1 - side], swap_recv.at[c], ssp.at[c], rsp.at[c],
+            device_id={"grp": partner}, device_id_type=pl.DeviceIdType.MESH,
+        )
+
+    def part_copy(k, c):
+        return pltpu.make_async_remote_copy(
+            pair_send.at[c], pair_recv.at[k, c], ssp.at[k * PARTS + c], rsp.at[k * PARTS + c],
+            device_id={"grp": lax.rem(mg + 2 * k, G)}, device_id_type=pl.DeviceIdType.MESH,
+        )
+
+    def gp_copy(c):
+        return pltpu.make_async_remote_copy(
+            gp.at[c, side], gp.at[c, side], ssg.at[c], rsg.at[c],
+            device_id={"grp": partner}, device_id_type=pl.DeviceIdType.MESH,
+        )
+
+    piece = hidden // PARTS
+    for c in range(PARTS):
+        partial = mm(features, w[:, c * piece : (c + 1) * piece])
+        for g in range(G):
+            block = partial[g * share : (g + 1) * share]
+            part_f32[c, g % 2, g // 2] = block
+            part_send[c, g % 2, g // 2] = block.astype(BF16)
+        swap(c).start()
+    for c in range(PARTS):
+        swap(c).wait_recv()
+        pair = part_f32[c, side] + swap_recv[c].astype(F32)
+        pair_send[c] = pair.astype(BF16)
+        for k in range(1, half):
+            part_copy(k, c).start()
+        part_f32[c, side] = pair + b_ref[:, c * piece : (c + 1) * piece]
+    logits = jnp.zeros((half * share, 1), F32)
+    slopes = []
+    for c in range(PARTS):
+        pre = part_f32[c, side]
+        for k in range(1, half):
+            part_copy(k, c).wait_recv()
+            pre = pre + pair_recv[k, c].astype(F32)
+        pre = pre.reshape(half * share, piece)
+        sig = jax.nn.sigmoid(pre)
+        w_out = wo_ref[:, c * piece : (c + 1) * piece]
+        logits = logits + jnp.sum(pre * sig * w_out, axis=1, keepdims=True)
+        slopes.append(w_out * (sig * (1.0 + pre * (1.0 - sig))))
     targets = jnp.concatenate(
         [
             col[pl.ds(pl.multiple_of((2 * j + side) * share, share), share), 2:3]
@@ -281,37 +389,33 @@
         axis=0,
     ).astype(F32)
     grad_logit = jax.nn.sigmoid(logits) - targets
-    grad_half = (grad_logit * w_out * (sig * (1.0 + pre * (1.0 - sig)))).astype(BF16)
-    gp[side] = grad_half.reshape(half, share, hidden)
-    gp_copy = pltpu.make_async_remote_copy(
-        gp.at[side], gp.at[side], ssg.at[0], rsg.at[0],
-        device_id={"grp": partner}, device_id_type=pl.DeviceIdType.MESH,
-    )
-    gp_copy.start()
+    for c in range(PARTS):
+        gp[c, side] = (grad_logit * slopes[c]).astype(BF16).reshape(half, share, piece)
+        gp_copy(c).start()
     losses = (
         jnp.maximum(logits, 0.0) + jnp.log1p(jnp.exp(-jnp.abs(logits))) - targets * logits
     )
     diag = iota((half * share, share), 0) - mine * share == iota((half * share, share), 1)
     loss_ref[...] = jnp.sum(jnp.where(diag, losses, 0.0), axis=0, keepdims=True)
-    gp_copy.wait_recv()
-    grad_pre = jnp.concatenate([gp[g % 2, g // 2] for g in range(G)], axis=0)
-
-    grad_emb = lax.dot_general(
-        grad_pre, w[...], (((1,), (1,)), ((), ())),
-        preferred_element_type=F32,
-    )
-    grad_rows = jnp.concatenate(
-        [grad_emb[:, f * emb : (f + 1) * emb] for f in range(fgrp)], axis=0
-    )
-    rg[0] = (grad_rows * looked[1]).astype(BF16)
-    rg[1] = (grad_rows * looked[0]).astype(BF16)
-    rg[2] = grad_rows.astype(BF16)
+
+    grad_emb = None
+    for c in range(PARTS):
+        gp_copy(c).wait_recv()
+        grad_pre = jnp.concatenate([gp[c, g % 2, g // 2] for g in range(G)], axis=0)
+        term = mm(grad_pre, w_t[c * piece : (c + 1) * piece, :])
+        grad_emb = term if grad_emb is None else grad_emb + term
+    for f in range(fgrp):
+        at = pl.ds(f * bdev, bdev)
+        grad_rows = grad_emb[:, f * emb : (f + 1) * emb]
+        rg[0, at, :] = (grad_rows * looked[1, at, :]).astype(BF16)
+        rg[1, at, :] = (grad_rows * looked[0, at, :]).astype(BF16)
+        rg[2, at, :] = grad_rows.astype(BF16)
 
     def collect(dst):
         at = pl.ds(pl.multiple_of(dst * width, width), width)
         g_send[dst] = joined([mm(pt_ref[t, at, :], rg[t]) for t in range(3)])
 
-    g_start, g_wait, g_drain = exchange(collect, g_send, g_recv, ss2, rs2, up)
+    g_start, g_wait, g_drain = exchange(collect, g_send, g_recv, ss2, rs2, False)
     g_start()
 
     @pl.loop(1, R)
@@ -319,10 +423,17 @@
         req_copy(k).wait_send()
 
     rows_drain()
-    swap.wait_send()
-    gp_copy.wait_send()
-    for k in range(1, half):
-        part_copy(k).wait_send()
+    if paired:
+        @pl.when(inner == 1)
+        def _():
+            for j in range(3):
+                dense_copy(j).wait_send()
+
+    for c in range(PARTS):
+        swap(c).wait_send()
+        gp_copy(c).wait_send()
+        for k in range(1, half):
+            part_copy(k, c).wait_send()
 
     for n in range(CHUNKS):
         g_wait(n)
@@ -331,6 +442,17 @@
             tg_ref[t] = part if n == 0 else tg_ref[t] + part
 
     g_drain()
+
+
+def store(tg_ref, loss_ref, tg_out, loss_out, sem):
+    copies = (
+        pltpu.make_async_copy(tg_ref, tg_out, sem.at[0]),
+        pltpu.make_async_copy(loss_ref, loss_out, sem.at[1]),
+    )
+    for copy in copies:
+        copy.start()
+    for copy in copies:
+        copy.wait()
 
 
 def body(owner, offset, tables, w_first, b_first, w_out, labels):
@@ -352,6 +474,7 @@
     share = bdev // G
     half = G // 2
     slots = R * width
+    piece = hidden // PARTS
 
     owner_rows = owner.transpose(1, 2, 0)
     offset_rows = offset.transpose(1, 2, 0)
@@ -371,6 +494,7 @@
             pltpu.VMEM((3, n_rows, emb), F32),
             pltpu.VMEM((3, n_rows, emb), BF16),
             pltpu.VMEM(w_first.shape, BF16),
+            pltpu.VMEM((hidden, fgrp * emb), BF16),
             pltpu.VMEM((nl, 8), jnp.int32),
             pltpu.VMEM((nl, n_rows), BF16),
             pltpu.VMEM((R * 8, n_rows), BF16),
@@ -378,22 +502,25 @@
             pltpu.VMEM((R, 4, n_rows), BF16),
             pltpu.VMEM((R, total, emb), BF16),
             pltpu.VMEM((R, total, emb), BF16),
+            pltpu.VMEM((2, n_rows if R == 2 * CHUNKS else 16, emb), BF16),
+            pltpu.VMEM((per if R == 2 * CHUNKS else 8, emb), F32),
             pltpu.VMEM((3, per, emb), F32),
             pltpu.VMEM((3, CHUNKS, per, slots // CHUNKS), BF16),
             pltpu.VMEM((3, slots, per), BF16),
             pltpu.VMEM((3, CHUNKS, n_rows, slots // CHUNKS), BF16),
-            pltpu.VMEM((2, half, share, hidden), F32),
-            pltpu.VMEM((2, half, share, hidden), BF16),
-            pltpu.VMEM((half, share, hidden), BF16),
-            pltpu.VMEM((half, share, hidden), BF16),
-            pltpu.VMEM((half, half, share, hidden), BF16),
-            pltpu.VMEM((2, half, share, hidden), BF16),
+            pltpu.VMEM((PARTS, 2, half, share, piece), F32),
+            pltpu.VMEM((PARTS, 2, half, share, piece), BF16),
+            pltpu.VMEM((PARTS, half, share, piece), BF16),
+            pltpu.VMEM((PARTS, half, share, piece), BF16),
+            pltpu.VMEM((half, PARTS, half, share, piece), BF16),
+            pltpu.VMEM((PARTS, 2, half, share, piece), BF16),
             pltpu.VMEM((3, per, emb), BF16),
             pltpu.VMEM((R, total, emb), BF16),
             pltpu.VMEM((R, total, emb), BF16),
             sems((2,)),
             sems((R,)), sems((R,)), sems((R,)), sems((R,)), sems((R,)), sems((R,)),
-            sems((G,)), sems((G,)), sems((G,)), sems((G,)),
+            sems((4,)), sems((2,)),
+            sems((half * PARTS,)), sems((half * PARTS,)), sems((PARTS,)), sems((PARTS,)),
         ],
         compiler_params=pltpu.CompilerParams(
             collective_id=0, has_side_effects=True, vmem_limit_bytes=(44 if slots <= 1024 else 60) * MIB
@@ -408,6 +535,18 @@
             )
         )
     )
+    table_grad, losses = pl.pallas_call(
+        store,
+        out_shape=(
+            jax.ShapeDtypeStruct((3, n_rows, emb), F32),
+            jax.ShapeDtypeStruct((1, share), F32),
+        ),
+        in_specs=[vmem, vmem],
+        out_specs=(hbm, hbm),
+        scratch_shapes=[sems((2,))],
+        compiler_params=pltpu.CompilerParams(vmem_limit_bytes=MIB),
+        name="store",
+    )(table_grad, losses)
     return table_grad, losses.reshape(share)
 
 

time: 54 us -> 52.9 us (0.980)
  local copies, waits for them, and re-layouts: 1.39 us -> 0 us
    unnamed x2 -> x0, local copies, waits for them, and re-layouts: 1.39 us -> none
    pallas_call x0 -> x1, Pallas kernels: none -> 0.9 us  [body(): pl.pallas_call(store, out_shape=(jax.ShapeDtypeStruct((3, n_rows, emb), F...]
    pallas_call x1, Pallas kernels: 51.7 us -> 51.1 us  [body(): pl.pallas_call(functools.partial(kernel, R, G, cap, fgrp, starts, width),...]
where the time goes in v2:
time: 52.9 us; the launch traced here: 52.7 us
  Pallas kernels  52 us (98%)
  between operations  0.64 us (1%)
    pallas_call x1, Pallas kernels, body(): pl.pallas_call(functools.partial(kernel, R, G, cap, fgrp, starts, width),...  51.1 us

profile of v2, /device:TPU:13, one launch (start us, length us, event | category | flops | bytes accessed | tf_op | source)
XLA Modules:
  0.0 52.7 jit_solution(3219439606961485563)
XLA Ops:
  0.6 51.1 %embed_step.1 = (f32[3,512,128]{2,1,0:T(8,128)S(1)}, f32[1,32]{1,0:T(1,128)S(1)}) custom-call(s32[6,3,128]{2,1,0:T(4,128)} %bitcast.6, s32[6,3,128]{2,1,0:T(4,128)} %bitcast.7, s32[1,128]{1,0:T(1,128)} %bitcast.10, f32[3,512,128]{2,1,0:T(8,128)} %tab_hbm.1, bf16[768,1024]{1,0:T(8,128)(2,1)} %w_hbm.1, f32[1,1024]{1,0:T(1,128)} %bitcast.8, f32[1,1024]{1,0:T(1,128)} %bitcast.9), custom_call_target="tpu_custom_call" | custom-call | tf_op jit(solution)/shard_map/embed_step/pallas_call | solution.py:484
  51.8 0.9 %store.1 = (f32[3,512,128]{2,1,0:T(8,128)}, f32[1,32]{1,0:T(1,128)}) custom-call(f32[3,512,128]{2,1,0:T(8,128)S(1)} %get-tuple-element.6.tg_ref, f32[1,32]{1,0:T(1,128)S(1)} %get-tuple-element.7.loss_ref), custom_call_target="tpu_custom_call" | custom-call | tf_op jit(solution)/shard_map/store/pallas_call | solution.py:538

commit v3 on v2

--- a/solution.py
+++ b/solution.py
@@ -10,8 +10,8 @@
 BF16 = jnp.bfloat16
 F32 = jnp.float32
 CHUNKS = 4
-PARTS = 2
-DENSE_AT = 1
+PARTS = 1
+DENSE_AT = 2
 MIB = 1024 * 1024
 
 
@@ -83,7 +83,7 @@
     def nth_chunk(n):
         if not paired:
             return lax.rem(my_chunk + n, CHUNKS)
-        return (my_chunk, pair_chunk, 3 - 3 * my_half, far_inner)[n]
+        return (my_chunk, 3 - 3 * my_half, pair_chunk, far_inner)[n]
 
     def is_inner(z):
         return lax.rem(lax.div(z + 1, 2), 2)

time: 52.9 us -> 51.7 us (0.977)
  Pallas kernels: 52 us -> 50.8 us
    pallas_call x1, Pallas kernels: 51.1 us -> 49.9 us  [body(): pl.pallas_call(functools.partial(kernel, R, G, cap, fgrp, starts, width),...]
where the time goes in v3:
time: 51.7 us; the launch traced here: 51.4 us
  Pallas kernels  50.8 us (98%)
  between operations  0.64 us (1%)
    pallas_call x1, Pallas kernels, body(): pl.pallas_call(functools.partial(kernel, R, G, cap, fgrp, starts, width),...  49.9 us

profile of v3, /device:TPU:13, one launch (start us, length us, event | category | flops | bytes accessed | tf_op | source)
XLA Modules:
  0.0 51.4 jit_solution(18073669999440215750)
XLA Ops:
  0.6 49.9 %embed_step.1 = (f32[3,512,128]{2,1,0:T(8,128)S(1)}, f32[1,32]{1,0:T(1,128)S(1)}) custom-call(s32[6,3,128]{2,1,0:T(4,128)} %bitcast.6, s32[6,3,128]{2,1,0:T(4,128)} %bitcast.7, s32[1,128]{1,0:T(1,128)} %bitcast.10, f32[3,512,128]{2,1,0:T(8,128)} %tab_hbm.1, bf16[768,1024]{1,0:T(8,128)(2,1)} %w_hbm.1, f32[1,1024]{1,0:T(1,128)} %bitcast.8, f32[1,1024]{1,0:T(1,128)} %bitcast.9), custom_call_target="tpu_custom_call" | custom-call | tf_op jit(solution)/shard_map/embed_step/pallas_call | solution.py:484
  50.5 0.9 %store.1 = (f32[3,512,128]{2,1,0:T(8,128)}, f32[1,32]{1,0:T(1,128)}) custom-call(f32[3,512,128]{2,1,0:T(8,128)S(1)} %get-tuple-element.6.tg_ref, f32[1,32]{1,0:T(1,128)S(1)} %get-tuple-element.7.loss_ref), custom_call_target="tpu_custom_call" | custom-call | tf_op jit(solution)/shard_map/store/pallas_call | solution.py:538

commit v4 on v3

--- a/solution.py
+++ b/solution.py
@@ -218,6 +218,8 @@
     ranked_bf[...] = ranked.astype(BF16)
     req_send[...] = ranked.reshape(R, 8, n_rows)[:, 0:4].astype(BF16)
 
+    tab_copy.wait()
+    tb[...] = tab[...].astype(BF16)
     pl.semaphore_wait(barrier, R - 1 + G - 1)
 
     def req_copy(k):
@@ -236,8 +238,6 @@
     def _(k):
         req_copy(k).start()
 
-    tab_copy.wait()
-    tb[...] = tab[...].astype(BF16)
     if paired:
         @pl.when(inner == 1)
         def _():

time: 51.7 us -> 51.7 us (level)
  no operation moved by 1% of the time
where the time goes in v4:
time: 51.7 us; the launch traced here: 51.4 us
  Pallas kernels  50.8 us (98%)
  between operations  0.64 us (1%)
    pallas_call x1, Pallas kernels, body(): pl.pallas_call(functools.partial(kernel, R, G, cap, fgrp, starts, width),...  49.9 us

profile of v4, /device:TPU:13, one launch (start us, length us, event | category | flops | bytes accessed | tf_op | source)
XLA Modules:
  0.0 51.4 jit_solution(448393225349806304)
XLA Ops:
  0.6 49.9 %embed_step.1 = (f32[3,512,128]{2,1,0:T(8,128)S(1)}, f32[1,32]{1,0:T(1,128)S(1)}) custom-call(s32[6,3,128]{2,1,0:T(4,128)} %bitcast.6, s32[6,3,128]{2,1,0:T(4,128)} %bitcast.7, s32[1,128]{1,0:T(1,128)} %bitcast.10, f32[3,512,128]{2,1,0:T(8,128)} %tab_hbm.1, bf16[768,1024]{1,0:T(8,128)(2,1)} %w_hbm.1, f32[1,1024]{1,0:T(1,128)} %bitcast.8, f32[1,1024]{1,0:T(1,128)} %bitcast.9), custom_call_target="tpu_custom_call" | custom-call | tf_op jit(solution)/shard_map/embed_step/pallas_call | solution.py:484
  50.5 0.9 %store.1 = (f32[3,512,128]{2,1,0:T(8,128)}, f32[1,32]{1,0:T(1,128)}) custom-call(f32[3,512,128]{2,1,0:T(8,128)S(1)} %get-tuple-element.6.tg_ref, f32[1,32]{1,0:T(1,128)S(1)} %get-tuple-element.7.loss_ref), custom_call_target="tpu_custom_call" | custom-call | tf_op jit(solution)/shard_map/store/pallas_call | solution.py:538
